TPU v7x, 32 devices: a 4x4x1 block of a 4x4x8 slice. The times are simulated.
32 devices in a mesh: batch: 1 (over z), row: 4 (over y), col: 8 (over x, core).
Axes of the slice: x: 4, y: 4, z: 1, core: 2. Of those that a mesh axis runs over, the one named last changes fastest.
The devices are a block of a 4x4x8 slice.
Arguments:
- left_op: bfloat16 [16384, 16384], P(('batch', 'row'), 'col')
- left_start: float32 [16384, 256], P(('batch', 'row', 'col'))
- right_op: bfloat16 [16384, 16384], P(('batch', 'row'), 'col')
- right_start: float32 [16384, 256], P(('batch', 'row', 'col'))
Outputs:
- output 1: float32 [16384, 256], P(('batch', 'row', 'col'))
- output 2: float32 [256, 256], P('batch')
- output 3: float32 [16384, 256], P(('batch', 'row', 'col'))
- output 4: float32 [256, 256], P('batch')
All inputs are finite; a program needn't handle non-finite values.
Results may differ from a plain program's by a relative error of at most 0.001.
Values are sent between devices in bfloat16 or wider.
A program may use at most 768 MiB of HBM per device.

v0:
```python
import functools

import jax
import jax.numpy as jnp
from jax import lax
from jax.experimental import pallas as pl
from jax.experimental.pallas import tpu as pltpu
from jax.sharding import PartitionSpec as P

SWEEPS = 4
CORES = 2
RING = 4
PIVOTS = 32
STEP = 16
AHEAD = 2
LEFT_PARTS, RIGHT_PARTS = (2, 0, 1, 1, 0, 0), (0, 2, 1, 0, 1, 0)
GROUP = 8
VMEM_BYTES = 67043328
F32, BF16 = jnp.float32, jnp.bfloat16
TN = (((0,), (0,)), ((), ()))
NT = (((1,), (1,)), ((), ()))

SLOTS = 8
KINDS = range(0, 17 * SLOTS, SLOTS)
AG_T, AG_A, AG_B, RELAY, RELAY_A, RS_T, RS_A, PAIR, GRAM_PAIR, GRAM_RS, GRAM_AG, LINV, MOVE, START, SWAP_Y, SWAP_H, DIAGONAL = KINDS
ORDER = (0, 2, 1, 3)
OFFSETS = sorted(
    ((dy, dx) for dy in range(RING) for dx in range(RING) if dy or dx),
    key=lambda o: -min(o[0], RING - o[0]) - min(o[1], RING - o[1]),
)


def split3(v):
    high = v.astype(BF16)
    rest = v - high.astype(F32)
    mid = rest.astype(BF16)
    return high, mid, (rest - mid.astype(F32)).astype(BF16)


def halves_dot(lhs, rhs, dims):
    axis = 1 - dims[0][0][0]
    size = lhs.shape[axis] // 2
    parts = [lax.slice_in_dim(lhs, i * size, (i + 1) * size, axis=axis) for i in range(2)]
    return jnp.concatenate([lax.dot_general(part, rhs, dims, preferred_element_type=F32) for part in parts], axis=0)


def dot_f32(lhs, rhs, dims):
    left, right = split3(lhs), split3(rhs)
    (lk,), (rk,) = dims[0]
    lhs = jnp.concatenate([left[i] for i in LEFT_PARTS], axis=lk)
    rhs = jnp.concatenate([right[i] for i in RIGHT_PARTS], axis=rk)
    return halves_dot(lhs, rhs, dims)


def gram_f32(v):
    high, mid, low = split3(v)
    mixed = halves_dot(jnp.concatenate([high, high], axis=0), jnp.concatenate([low, mid], axis=0), TN)
    return (halves_dot(mid, mid, TN) + (mixed + mixed.T)) + halves_dot(high, high, TN)


class Phases:
    def __init__(self):
        self.scope = None

    def __call__(self, name=None):
        if self.scope is not None:
            self.scope.__exit__(None, None, None)
        self.scope = None
        if name is not None:
            self.scope = jax.named_scope(name)
            self.scope.__enter__()


def rows_of(ref, part, parts=2):
    size = ref.shape[0] // parts
    return ref.at[pl.ds(part * size, size)]


def set_identity(work):
    width = work.shape[0]
    at_row = lax.broadcasted_iota(jnp.int32, (width, width), 0)
    at_col = lax.broadcasted_iota(jnp.int32, (width, width), 1)
    work[:, width : 2 * width] = jnp.where(at_row == at_col, 1.0, 0.0).astype(F32)


def inverse_factor(gram, diagonal, work, store):
    tile = gram.shape[1]
    width = 2 * tile
    at_row, at_col = (lax.broadcasted_iota(jnp.int32, (tile, tile), i) for i in range(2))
    packed = gram[0:tile]
    turned = packed.T
    work[0:tile, 0:tile] = jnp.where(at_row <= at_col, packed, turned)
    work[0:tile, tile:width] = gram[tile : 2 * tile]
    work[tile:width, tile:width] = jnp.where(at_row == at_col, diagonal, jnp.where(at_row > at_col, packed, turned))
    sub = lax.broadcasted_iota(jnp.int32, (GROUP, tile), 0)
    groups = PIVOTS // GROUP
    full = (GROUP, tile)

    def lane(row):
        return jnp.broadcast_to(row, full)

    for first in range(0, width, PIVOTS):
        near = first // tile
        gram_tiles = list(range(near, 2))
        tiles = gram_tiles + [2 + i for i in range(near + 1)]
        data = {
            t: [work[pl.ds(first + GROUP * g, GROUP), t * tile : (t + 1) * tile] for g in range(groups)] for t in tiles
        }
        pivots = [jnp.ones(full, F32) for _ in range(groups)]
        def spread_columns(start, end):
            at = first - near * tile
            return {
                j: {g: jnp.broadcast_to(data[near][g][:, at + j : at + j + 1], full) for g in range(j // GROUP, groups)}
                for j in range(start, end)
            }

        cols = spread_columns(0, STEP)
        for j in range(PIVOTS):
            if j == STEP - AHEAD:
                cols |= spread_columns(STEP, PIVOTS)
            gj, rj = divmod(j, GROUP)
            col = cols[j]
            pivot = lane(col[gj][rj : rj + 1])
            inv = 1.0 / pivot
            pivots[gj] = jnp.where(sub == rj, pivot, pivots[gj])
            for nxt in range(j + 1, PIVOTS if j >= STEP - AHEAD else STEP):
                gn, rn = divmod(nxt, GROUP)
                entry = lane(col[gn][rn : rn + 1])
                if nxt == j + 1:
                    for g in range(gn, groups):
                        cols[nxt][g] = cols[nxt][g] - (col[g] * entry) * inv
                else:
                    scaled = entry * inv
                    for g in range(gn, groups):
                        cols[nxt][g] = cols[nxt][g] - col[g] * scaled
            for g in range(gj, groups):
                factor = col[g] * inv
                if g == gj:
                    if rj == GROUP - 1:
                        continue
                    factor = jnp.where(sub > rj, factor, 0.0)
                for t in tiles:
                    data[t][g] = data[t][g] - factor * lane(data[t][gj][rj : rj + 1])
        scale = [lax.rsqrt(p) for p in pivots]
        for t in tiles:
            data[t] = [d * s for d, s in zip(data[t], scale, strict=True)]
        for t in tiles:
            if t >= 2:
                for g in range(groups):
                    store(first + GROUP * g, t - 2, data[t][g])
        nxt = first + PIVOTS
        if nxt == width:
            break
        parts = {t: split3(jnp.concatenate(data[t], axis=0)) for t in tiles}
        below = [t for t in gram_tiles if (t + 1) * tile > nxt]
        low = below[0] * tile
        lhs = jnp.concatenate([jnp.concatenate([parts[t][i] for i in LEFT_PARTS], axis=0) for t in below], axis=1)
        right_tiles = below + [t for t in tiles if t >= 2]
        rhs = jnp.concatenate([jnp.concatenate([parts[t][i] for i in RIGHT_PARTS], axis=0) for t in right_tiles], axis=1)
        upd = lax.dot_general(lhs, rhs, TN, preferred_element_type=F32)
        for n, t in enumerate(right_tiles):
            where = pl.ds(nxt, width - nxt), slice(t * tile, (t + 1) * tile)
            work[where] = work[where] - upd[nxt - low :, n * tile : (n + 1) * tile]


def kernel(
    sizes, left_op, left_start, right_op, right_start, x_out, h_out,
    ops, ycur, y_one, ag_t, ag_a, p_t, p_a, d_a, r_t, r_a, x_half, x_via, x_move, y_in, g_loc, g_pair, g_sum, g_in, g_red, g_all, h_all, d_all, work, linv,
    send, recv, load_sem,
):
    nrow, ncol, total_rows = sizes
    sub, width = ycur.shape[1:]
    tile, hsub = width // 2, sub // 2
    nchips = RING * RING
    y = lax.axis_index("row")
    c = lax.axis_index("col")
    x, k = lax.div(c, CORES), lax.rem(c, CORES)
    other = 1 - k
    xp, xm, xf = (lax.rem(x + d, RING) for d in (1, 3, 2))
    yp, ym, yf = (lax.rem(y + d, RING) for d in (1, 3, 2))

    def dev(row, chip, core):
        return {"row": row, "col": chip * CORES + core}

    partner = dev(y, x, other)

    def push(i, src, dst, to):
        return pltpu.make_async_remote_copy(
            src_ref=src, dst_ref=dst, send_sem=send.at[i], recv_sem=recv.at[i], device_id=to, device_id_type=pl.DeviceIdType.MESH
        )

    def spot(i):
        return lax.rem(i + RING - x, RING)

    def run(index, size):
        return pl.ds(pl.multiple_of(index * size, size), size)

    phase = Phases()
    phase("boot")
    barrier = pltpu.get_barrier_semaphore()
    here = y * ncol + c
    for o in range(1, nrow * ncol):
        there = lax.rem(here + o, nrow * ncol)
        pl.semaphore_signal(
            barrier, inc=1, device_id={"row": lax.div(there, ncol), "col": lax.rem(there, ncol)}, device_id_type=pl.DeviceIdType.MESH
        )

    starts = [
        pltpu.make_async_copy(left_start, ycur.at[0], load_sem.at[8]),
        pltpu.make_async_copy(right_start, ycur.at[1], load_sem.at[9]),
    ]
    loads_t, loads_a = [], []
    for n, (xi, yi) in enumerate(((x, y), (xm, ym), (xp, yp), (xf, yf))):
        take = run(xi, CORES * sub)
        loads_t.append(pltpu.make_async_copy(left_op.at[take], ops.at[0, take], load_sem.at[2 * n]))
        take = run(spot(yi), sub)
        loads_a.append(pltpu.make_async_copy(right_op.at[:, take], ops.at[1, :, take], load_sem.at[2 * n + 1]))
    for copy in starts + loads_t + loads_a:
        copy.start()

    shift = CORES * lax.rem(x, 2) + k
    behind = spot(y)
    up, down = lax.rem(y + shift, RING), lax.rem(y + RING - shift, RING)

    def move(i, src, dst, row, chip, core):
        stays = jnp.logical_and(row == y, jnp.logical_and(chip == x, core == k))
        return push(i, src, dst, dev(row, chip, core)), stays, src, dst

    def start_moves(*moves):
        for copy, stays, src, dst in moves:

            @pl.when(stays)
            def _():
                dst[...] = src[...]

            @pl.when(jnp.logical_not(stays))
            def _():
                copy.start()

    def end_moves(*moves):
        for copy, stays, _, _ in moves:

            @pl.when(jnp.logical_not(stays))
            def _():
                copy.wait()

    for copy in starts:
        copy.wait()
    for h in range(2):
        ag_t[x, h, k] = ycur[0, h * hsub : (h + 1) * hsub].T.astype(BF16)
    for h in range(2):
        x_half[0, h] = ycur[1, h * hsub : (h + 1) * hsub].astype(BF16)
    pl.semaphore_wait(barrier, nrow * ncol - 1)
    first_one = [move(MOVE + h, x_half.at[0, h], x_half.at[1, h], up, x, k) for h in range(2)]
    first_two = [move(MOVE + 2 + h, x_half.at[1, h], ag_a.at[y, h], y, down, lax.div(x, 2)) for h in range(2)]
    start_moves(*first_one)
    first_swap = [push(START + h, ag_t.at[x, h, k], ag_t.at[x, h, k], partner) for h in range(2)]
    for copy in first_swap:
        copy.start()
    phase()

    def piece_t(chip, h):
        return ag_t.at[chip, h]

    def gather_t():
        to_p, to_m = dev(y, xp, k), dev(y, xm, k)
        sends = [
            push(AG_T + n, piece_t(x, h), piece_t(x, h), to) for n, (h, to) in enumerate(((0, to_p), (1, to_p), (1, to_m), (0, to_m)))
        ]
        onward = [
            push(AG_T + 4, piece_t(xm, 0), piece_t(xm, 0), to_p),
            push(AG_T + 5, piece_t(xp, 1), piece_t(xp, 1), to_m),
        ]
        relays = [push(RELAY, ag_t.at[x], ag_t.at[x], partner)] + [
            push(RELAY + 1 + n, piece_t(i, h), piece_t(i, h), partner)
            for n, (i, h) in enumerate(((xm, 0), (xp, 1), (xm, 1), (xp, 0), (xf, 0), (xf, 1)))
        ]
        return sends, onward, relays

    def gather_a():
        routes = ((0, yp), (1, yp), (1, ym), (0, ym))
        sends = [push(AG_A + n, ag_a.at[y, h], ag_a.at[y, h], dev(i, x, k)) for n, (h, i) in enumerate(routes)]
        onward = [
            push(AG_A + 4, ag_a.at[ym, 0], ag_a.at[ym, 0], dev(yp, x, k)),
            push(AG_A + 5, ag_a.at[yp, 1], ag_a.at[yp, 1], dev(ym, x, k)),
        ]
        for_other = [
            pltpu.make_async_remote_copy(
                src_ref=x_half.at[0, h], dst_ref=ag_a.at[y, h], send_sem=send.at[AG_B + n], recv_sem=recv.at[AG_A + n],
                device_id=dev(i, x, other), device_id_type=pl.DeviceIdType.MESH,
            )
            for n, (h, i) in enumerate(routes)
        ]
        return sends, onward, for_other, push(RELAY_A, x_half.at[0], ag_a.at[y], partner)

    def ring_scatter(base, part, got, plus, minus, far, to):
        def half(i, h):
            return rows_of(part(i), h)

        return [
            push(base + 0, half(far, 0), got.at[0], to(plus)),
            push(base + 1, half(far, 1), got.at[1], to(minus)),
            push(base + 2, half(plus, 1), got.at[2], to(plus)),
            push(base + 3, half(minus, 0), got.at[3], to(minus)),
            push(base + 4, half(plus, 0), got.at[4], to(plus)),
            push(base + 5, half(minus, 1), got.at[5], to(minus)),
        ]

    step_one = [
        move(MOVE, ycur.at[0], x_via.at[0], up, x, k),
        move(MOVE + 1, ycur.at[1], x_via.at[1], y, CORES * k + lax.div(behind, 2), lax.rem(behind, 2)),
    ]
    step_two = [
        move(MOVE + 2, x_via.at[0], x_move.at[0], y, down, lax.div(x, 2)),
        move(MOVE + 3, x_via.at[1], x_move.at[1], down, x, k),
    ]
    out_left = pltpu.make_async_copy(x_via.at[0], x_out.at[0], load_sem.at[0])
    out_right = pltpu.make_async_copy(x_move.at[1], x_out.at[1], load_sem.at[1])

    def share_linv(q):
        return push(LINV + q, linv.at[q, k], linv.at[q, k], partner)

    swap_y = push(SWAP_Y, ycur.at[other], y_in, partner)

    def apply(p):
        t = lax.rem(p, 2)
        a = 1 - t

        def mm_t(pieces, owner, first=False, cuts=1):
            size = sub // cuts
            for n in range(cuts):
                acc, lanes = None, slice(n * size, (n + 1) * size)
                for chip, h in pieces:
                    for core in range(CORES):
                        rows = run((chip * CORES + core) * 2 + h, hsub)
                        one = jnp.dot(ag_t[chip, h, core], ops[t, rows, run(spot(owner) * cuts + n, size)], preferred_element_type=F32)
                        acc = one if acc is None else acc + one
                p_t[owner, :, lanes] = acc if first else p_t[owner, :, lanes] + acc

        def mm_a(pieces, owner, first=False, cuts=1):
            size = sub // cuts
            for n in range(cuts):
                acc, rows = None, slice(n * size, (n + 1) * size)
                for i, h in pieces:
                    one = jnp.dot(ops[a, run(owner * cuts + n, size), run(spot(i) * 2 + h, hsub)], ag_a[i, h], preferred_element_type=F32)
                    acc = one if acc is None else acc + one
                p_a[owner, rows] = acc if first else p_a[owner, rows] + acc

        def loaded(copy):
            @pl.when(p == 0)
            def _():
                copy.wait()

        send_t, fwd_t, relays = gather_t()
        send_a, fwd_a, send_b, relay_a = gather_a()
        drives_t, drives_a = k == t, k == a
        own_y = [(y, 0), (y, 1)]
        phase("ag_own")

        @pl.when(p == 0)
        def _():
            for h in range(2):
                end_moves(first_one[h])
                start_moves(first_two[h])
            for copy in first_swap:
                copy.wait()

            @pl.when(drives_t)
            def _():
                for n in ORDER:
                    send_t[n].start()

        @pl.when(p > 0)
        def _():
            @pl.when(jnp.logical_not(drives_a))
            def _():
                relay_a.wait_recv()

            for owner in range(RING * CORES):
                mm_a(own_y, owner, True)

            @pl.when(jnp.logical_not(drives_t))
            def _():
                relays[0].wait_recv()

        loaded(loads_t[0])
        for owner in range(RING):
            mm_t([(x, 0), (x, 1)], owner, True)

        @pl.when(p == 0)
        def _():
            end_moves(first_two[0])
            send_a[0].start()
            send_a[3].start()
            end_moves(first_two[1])
            send_a[2].start()
            send_a[1].start()
            loads_a[0].wait()
            for owner in range(RING * CORES):
                mm_a(own_y, owner, True)

        def take_t(arrived, then):
            @pl.when(drives_t)
            def _():
                for copy, follow in zip(arrived, then):
                    copy.wait_recv()
                    for nxt in follow:
                        nxt.start()

        def relayed(*copies):
            @pl.when(jnp.logical_not(drives_t))
            def _():
                for copy in copies:
                    copy.wait_recv()

        phase("ag_wait1")
        take_t([send_t[n] for n in ORDER[:2]], zip(fwd_t, relays[1:3]))
        for n, copy in zip(ORDER, fwd_a):
            send_a[n].wait_recv()
            copy.start()
        phase("mm_near1")
        loaded(loads_a[1])
        loaded(loads_a[2])
        for owner in range(RING * CORES):
            mm_a([(ym, 0), (yp, 1)], owner)
        relayed(*relays[1:3])
        loaded(loads_t[1])
        loaded(loads_t[2])
        for owner in range(RING):
            mm_t([(xm, 0), (xp, 1)], owner)
        phase("mm_near2")
        take_t([send_t[n] for n in ORDER[2:]], zip(relays[3:5]))
        for n in ORDER[2:]:
            send_a[n].wait_recv()
        for owner in range(RING * CORES):
            mm_a([(ym, 1), (yp, 0)], owner)
        relayed(*relays[3:5])
        for owner in range(RING):
            mm_t([(xm, 1), (xp, 0)], owner)
        phase("ag_far")
        take_t(fwd_t, zip(relays[5:]))
        for copy in fwd_a:
            copy.wait_recv()
        phase("mm_far")

        loaded(loads_a[3])
        pairs = []
        far_y = [(yf, 0), (yf, 1)]
        out_t = ring_scatter(RS_T, lambda i: p_t.at[i], r_t, yp, ym, yf, lambda i: dev(i, x, k))
        out_a = ring_scatter(RS_A, lambda i: p_a.at[i * CORES + k], r_a, xp, xm, xf, lambda i: dev(y, i, k))

        def pair(n, i, rows):
            pairs.append(push(PAIR + n, p_a.at[i * CORES + other, rows], d_a.at[i, rows], partner))
            pairs[n].start()

        def add_pair(n, i, rows):
            pairs[n].wait_recv()
            p_a[i * CORES + k, rows] = p_a[i * CORES + k, rows] + d_a[i, rows]

        every, half_rows = pl.ds(0, sub), [pl.ds(h * hsub, hsub) for h in range(2)]
        far_x = [(xf, 0), (xf, 1)]
        mm_a(far_y, xf * CORES + other, cuts=2)
        for h in range(2):
            pair(h, xf, half_rows[h])
        relayed(*relays[5:])
        loaded(loads_t[3])
        mm_t(far_x, yf, cuts=2)
        out_t[0].start()
        out_t[1].start()
        mm_a(far_y, xf * CORES + k, cuts=2)
        for h in range(2):
            add_pair(h, xf, half_rows[h])
            out_a[h].start()
        for n, i in enumerate((xp, xm, x)):
            mm_a(far_y, i * CORES + other)
        for n, i in enumerate((xp, xm, x)):
            pair(2 + n, i, every)
        mm_t(far_x, yp)
        mm_t(far_x, ym)
        out_t[2].start()
        out_t[3].start()
        for i in (xp, xm, x):
            mm_a(far_y, i * CORES + k)
        add_pair(2, xp, every)
        add_pair(3, xm, every)
        out_a[2].start()
        out_a[3].start()
        mm_t(far_x, y)
        phase("rs_mid")

        ht = width // 2
        out_t[0].wait_recv()
        p_t[yp, 0:ht] = p_t[yp, 0:ht] + r_t[0]
        out_t[4].start()
        out_t[1].wait_recv()
        p_t[ym, ht:width] = p_t[ym, ht:width] + r_t[1]
        out_t[5].start()
        out_a[0].wait_recv()
        kp, km, kk = xp * CORES + k, xm * CORES + k, x * CORES + k
        p_a[kp, 0:hsub] = p_a[kp, 0:hsub] + r_a[0]
        out_a[4].start()
        out_a[1].wait_recv()
        p_a[km, hsub:sub] = p_a[km, hsub:sub] + r_a[1]
        out_a[5].start()
        phase("rs_end")

        @pl.when(p == SWEEPS)
        def _():
            end_moves(*step_two)
            for q in range(2):
                share_linv(q).wait()
            for op in range(2):
                y_one[op] = dot_f32(x_move[op], linv[0, op], NT)
                x_move[op] = dot_f32(y_one[op], linv[1, op], NT)
            out_right.start()
            y_one[0] = dot_f32(ycur[0], linv[0, 0], NT)
            x_via[0] = dot_f32(y_one[0], linv[1, 0], NT)
            out_left.start()

        add_pair(4, x, every)
        for copy in out_t[2:] + out_a[2:]:
            copy.wait_recv()
        phase("rs_sum")
        ycur[t, :, 0:ht] = (p_t[y, 0:ht] + r_t[3] + r_t[4]).T
        ycur[t, :, ht:width] = (p_t[y, ht:width] + r_t[2] + r_t[5]).T
        ycur[a, 0:hsub] = p_a[kk, 0:hsub] + r_a[3] + r_a[4]
        ycur[a, hsub:sub] = p_a[kk, hsub:sub] + r_a[2] + r_a[5]
        phase("rs_drain")
        for copy in fwd_a + pairs + out_t + out_a:
            copy.wait_send()

        @pl.when(drives_t)
        def _():
            for copy in send_t + fwd_t + relays[1:]:
                copy.wait_send()

            @pl.when(p > 0)
            def _():
                relays[0].wait_send()

        @pl.when(jnp.logical_or(p == 0, drives_a))
        def _():
            for copy in send_a:
                copy.wait_send()

        @pl.when(jnp.logical_and(p > 0, drives_a))
        def _():
            for copy in send_b + [relay_a]:
                copy.wait_send()

        phase()

    def routes():
        for dy, dx in OFFSETS:
            to_y, to_x = (y, yp, yf, ym)[dy], (x, xp, xf, xm)[dx]
            yield dy * RING + dx, to_y * RING + to_x, to_y, to_x

    def pair_of(rows):
        return push(GRAM_PAIR, g_loc.at[other, pl.ds(0, rows)], g_pair.at[pl.ds(0, rows)], partner)

    def pair_sum(rows, local, behind=None):
        phase("ar_pair")
        local(other)
        pair = pair_of(rows)
        pair.start()
        local(k)
        pair.wait_recv()
        if behind is not None:
            behind.start()
        g_sum[0:rows] = g_loc[k, 0:rows] + g_pair[0:rows]
        phase()

    def all_reduce(rows, meanwhile=None):
        piece = rows // nchips

        def chunk(ref, q):
            return ref.at[pl.ds(pl.multiple_of(q * piece, GROUP), piece)]

        def count(copies):
            return g_all.at[pl.ds(0, copies * piece)]

        def await_copies(sem, copies):
            pltpu.make_async_copy(count(copies), count(copies), sem).wait()

        phase("ar_rs")
        mine = y * RING + x
        owner = CORES - 1

        def spread(o, q, to_y, to_x):
            pltpu.make_async_remote_copy(
                src_ref=chunk(g_sum, q), dst_ref=g_in.at[k, pl.ds(o * piece, piece)], send_sem=send.at[GRAM_RS],
                recv_sem=recv.at[GRAM_RS + k], device_id=dev(to_y, to_x, owner), device_id_type=pl.DeviceIdType.MESH,
            ).start()

        for route in routes():
            spread(*route)
        if meanwhile is not None:
            meanwhile()

        @pl.when(k == 0)
        def _():
            spread(0, mine, y, x)
            await_copies(send.at[GRAM_RS], nchips)
            phase("ar_ag")
            await_copies(recv.at[GRAM_AG], nchips)
            phase("ar_drain")

        @pl.when(k == 1)
        def _():
            def hand_out(i, src, q, to_y, to_x, core):
                pltpu.make_async_remote_copy(
                    src_ref=src, dst_ref=chunk(g_all, q), send_sem=send.at[GRAM_AG + i], recv_sem=recv.at[GRAM_AG],
                    device_id=dev(to_y, to_x, core), device_id_type=pl.DeviceIdType.MESH,
                ).start()

            await_copies(recv.at[GRAM_RS], nchips)
            total = g_in[0, 0:piece]
            for o in range(1, nchips):
                total = total + g_in[0, o * piece : (o + 1) * piece]
            g_red[0:piece] = total / total_rows
            for _, _, to_y, to_x in routes():
                hand_out(1, g_red.at[pl.ds(0, piece)], mine, to_y, to_x, 0)
            hand_out(1, g_red.at[pl.ds(0, piece)], mine, y, x, 0)
            phase("ar_ag")
            await_copies(recv.at[GRAM_RS + 1], nchips - 1)
            total = chunk(g_sum, mine)[...]
            for o in range(1, nchips):
                total = total + g_in[1, o * piece : (o + 1) * piece]
            chunk(g_all, mine)[...] = total / total_rows
            for _, _, to_y, to_x in routes():
                hand_out(0, chunk(g_all, mine), mine, to_y, to_x, 1)
            await_copies(recv.at[GRAM_AG], nchips - 1)
            phase("ar_drain")
            await_copies(send.at[GRAM_RS], nchips - 1)
            await_copies(send.at[GRAM_AG], nchips - 1)
            await_copies(send.at[GRAM_AG + 1], nchips)

        phase()

    corners = ((0, 0), (0, 1), (1, 1), (1, 0))

    def put_gram(into, full):
        at_row, at_col = (lax.broadcasted_iota(jnp.int32, (tile, tile), i) for i in range(2))
        low = full[tile:width, tile:width]
        into[0:tile] = jnp.where(at_row <= at_col, full[0:tile, 0:tile], low)
        into[tile : 2 * tile] = full[0:tile, tile:width]
        diagonal = jnp.sum(jnp.where(at_row == at_col, low, 0.0), axis=0, keepdims=True)
        into[2 * tile : 2 * tile + GROUP] = jnp.broadcast_to(diagonal, (GROUP, tile))

    def half_gram(op):
        half = ycur[op].astype(BF16)
        put_gram(g_loc.at[op], lax.dot_general(half, half, TN, preferred_element_type=F32))

    def normalize(p, q):
        @pl.when(q == 0)
        def _():
            pair_sum(2 * tile + GROUP, half_gram, swap_y)
            phase()

        @pl.when(q == 1)
        def _():
            phase("gram2")
            put_gram(g_sum, gram_f32(y_one[0]) + gram_f32(y_one[1]))
            phase()

        last = p == SWEEPS - 1

        def clear():
            own = d_all.at[q, y * RING + x]
            own[...] = g_sum[2 * tile : 2 * tile + 1]
            for _, _, to_y, to_x in routes():
                push(DIAGONAL + q, own, own, dev(to_y, to_x, k)).start()
            set_identity(work)
            linv[q, k, 0:tile, tile:width] = jnp.zeros((tile, tile), F32)


        all_reduce(2 * tile, clear)
        others = d_all.at[q, pl.ds(0, nchips - 1)]
        for sem in (recv, send):
            pltpu.make_async_copy(others, others, sem.at[DIAGONAL + q]).wait()

        @pl.when(q == 0)
        def _():
            pair_of(2 * tile + GROUP).wait_send()

        @pl.when(jnp.logical_and(last, q == 0))
        def _():
            start_moves(*step_one)

        @pl.when(jnp.logical_and(last, q == 1))
        def _():
            end_moves(*step_one)
            start_moves(*step_two)

        phase("chol")

        def store(first, t, value):
            linv[q, k, pl.ds(first, GROUP), t * tile : (t + 1) * tile] = value

        diagonal = d_all[q, 0]
        for chip in range(1, nchips):
            diagonal = diagonal + d_all[q, chip]
        inverse_factor(g_all, diagonal / total_rows, work, store)
        phase("mul")

        @pl.when(last)
        def _():
            share_linv(q).start()

        @pl.when(q == 0)
        def _():
            swap_y.wait()
            both = jnp.concatenate([ycur[k], y_in[...]], axis=0)
            y_one[...] = dot_f32(both, linv[0, k], NT).reshape(y_one.shape)

        phase()

    def launch(p):
        t = lax.rem(p, 2)

        def new_x(i):
            d_a[i] = dot_f32(y_one[i], linv[1, k], NT)
            return [d_a[i, h * hsub : (h + 1) * hsub] for h in range(2)]

        phase("launch")

        @pl.when(k == t)
        def _():
            sends, _, relays = gather_t()
            for i, core in enumerate((k, other)):
                for h, rows in enumerate(new_x(i)):
                    ag_t[x, h, core] = rows.T.astype(BF16)
            for n in ORDER:
                sends[n].start()
            relays[0].start()

        @pl.when(k != t)
        def _():
            sends, _, for_other, relay_a = gather_a()
            for h, rows in enumerate(new_x(0)):
                ag_a[y, h] = rows.astype(BF16)
            for n in ORDER:
                sends[n].start()
            for h, rows in enumerate(new_x(1)):
                x_half[0, h] = rows.astype(BF16)
            for n in ORDER:
                for_other[n].start()
            relay_a.start()

        phase()

    def sweep(p, carry):
        apply(p)

        @pl.when(p < SWEEPS)
        def _():
            def one(q, carry):
                normalize(p, q)
                return carry

            lax.fori_loop(0, 2, one, 0)
            launch(p + 1)

        return carry

    lax.fori_loop(0, SWEEPS + 1, sweep, 0)

    def rayleigh(op):
        full = dot_f32(x_move[op], ycur[op], TN)
        for n, (i, j) in enumerate(corners):
            g_loc[op, n * tile : (n + 1) * tile] = full[i * tile : (i + 1) * tile, j * tile : (j + 1) * tile]

    pair_sum(4 * tile, rayleigh)
    all_reduce(4 * tile)
    pair_of(4 * tile).wait_send()
    phase("h_swap")
    swap = push(SWAP_H, g_all, h_all, partner)
    swap.start()
    swap.wait()
    for n, (i, j) in enumerate(corners):
        rows, at = slice(n * tile, (n + 1) * tile), (slice(i * tile, (i + 1) * tile), slice(j * tile, (j + 1) * tile))
        for op in range(2):
            h_out[(op, *at)] = jnp.where(k == op, g_all[rows], h_all[rows])
    out_left.wait()
    out_right.wait()
    phase()


def hand_over(x_ref, h_ref, left_x, left_h, right_x, right_h, x_buf, h_buf, sem_in, sem_out):
    size = x_buf.shape[1] // 2
    routes = []
    for op, (x_to, h_to) in enumerate(((left_x, left_h), (right_x, right_h))):
        for h in range(2):
            rows = pl.ds(h * size, size)
            routes.append((x_ref.at[op, rows], x_buf.at[op, rows], x_to.at[rows]))
        routes.append((h_ref.at[op], h_buf.at[op], h_to))
    come = [pltpu.make_async_copy(src, buf, sem_in.at[n]) for n, (src, buf, _) in enumerate(routes)]
    go = [pltpu.make_async_copy(buf, dst, sem_out.at[n]) for n, (_, buf, dst) in enumerate(routes)]
    for copy in come:
        copy.start()
    for copy, nxt in zip(come, go):
        copy.wait()
        nxt.start()
    for copy in go:
        copy.wait()


def solution(mesh):
    nrow, ncol = mesh.shape["row"], mesh.shape["col"]
    assert nrow == RING and ncol == RING * CORES

    def local_program(left_op, left_start, right_op, right_start):
        rows, cols = left_op.shape
        sub, width = left_start.shape
        tile = width // 2
        vmem = pltpu.VMEM
        dma = pltpu.SemaphoreType.DMA
        basis, ray = jax.ShapeDtypeStruct((sub, width), F32), jax.ShapeDtypeStruct((width, width), F32)
        both_x, both_h = pl.pallas_call(
            functools.partial(kernel, (nrow, ncol, rows * nrow)),
            out_shape=[jax.ShapeDtypeStruct((2, sub, width), F32), jax.ShapeDtypeStruct((2, width, width), F32)],
            in_specs=[pl.BlockSpec(memory_space=pl.ANY)] * 4,
            out_specs=[pl.BlockSpec(memory_space=pl.ANY), pl.BlockSpec(memory_space=vmem)],
            scratch_shapes=[
                vmem((2, rows, cols), BF16),
                vmem((2, sub, width), F32),
                vmem((2, sub, width), F32),
                vmem((RING, 2, CORES, width, sub // 2), BF16),
                vmem((nrow, 2, sub // 2, width), BF16),
                vmem((nrow, width, sub), F32),
                vmem((ncol, sub, width), F32),
                vmem((RING, sub, width), F32),
                vmem((6, width // 2, sub), F32),
                vmem((6, sub // 2, width), F32),
                vmem((2, 2, sub // 2, width), BF16),
                vmem((2, sub, width), F32),
                vmem((2, sub, width), F32),
                vmem((sub, width), F32),
                vmem((2, 4 * tile, tile), F32),
                vmem((4 * tile, tile), F32),
                vmem((4 * tile, tile), F32),
                vmem((2, 4 * tile, tile), F32),
                vmem((4 * tile // (RING * RING), tile), F32),
                vmem((4 * tile, tile), F32),
                vmem((4 * tile, tile), F32),
                vmem((2, RING * RING, 1, tile), F32),
                vmem((width, 2 * width), F32),
                vmem((2, 2, width, width), F32),
                dma((KINDS.stop,)),
                dma((KINDS.stop,)),
                dma((10,)),
            ],
            compiler_params=pltpu.CompilerParams(collective_id=0, has_side_effects=True, vmem_limit_bytes=VMEM_BYTES),
            name="subspace",
        )(left_op, left_start, right_op, right_start)
        anywhere = pl.BlockSpec(memory_space=pl.ANY)
        return pl.pallas_call(
            hand_over,
            out_shape=[basis, ray, basis, ray],
            in_specs=[anywhere] * 2,
            out_specs=[anywhere] * 4,
            scratch_shapes=[vmem((2, sub, width), F32), vmem((2, width, width), F32), dma((6,)), dma((6,))],
            name="hand_over",
        )(both_x, both_h)

    op_spec = P(("batch", "row"), "col")
    vec_spec = P(("batch", "row", "col"), None)
    small_spec = P("batch", None)
    return jax.shard_map(
        local_program,
        mesh=mesh,
        in_specs=(op_spec, vec_spec, op_spec, vec_spec),
        out_specs=(vec_spec, small_spec, vec_spec, small_spec),
        check_vma=False,
    )
```

profile of v0, /device:TPU:97, one launch (start us, length us, event | category | flops | bytes accessed | tf_op | source)
XLA Modules:
  0.0 352.9 jit_solution(17978626836715190488)
XLA Ops:
  0.6 349.9 %subspace.1 = (f32[2,512,256]{2,1,0:T(8,128)}, f32[2,256,256]{2,1,0:T(8,128)}) custom-call(bf16[4096,2048]{1,0:T(8,128)(2,1)} %left_op.1, f32[512,256]{1,0:T(8,128)} %left_start.1, bf16[4096,2048]{1,0:T(8,128)(2,1)} %right_op.1, f32[512,256]{1,0:T(8,128)} %right_start.1), custom_call_target="tpu_custom_call" | custom-call | tf_op jit(solution)/shard_map/subspace/pallas_call | solution.py:819
  350.5 2.2 hand_over.1
where the time goes:
time: 353 us
  Pallas kernels  352 us (100%)
    pallas_call x1, Pallas kernels, local_program(): pl.pallas_call(functools.partial(kernel, (nrow, ncol, rows * nrow)), out_...  350 us

commit v1 on v0

--- a/solution.py
+++ b/solution.py
@@ -310,10 +310,13 @@
         move(MOVE, ycur.at[0], x_via.at[0], up, x, k),
         move(MOVE + 1, ycur.at[1], x_via.at[1], y, CORES * k + lax.div(behind, 2), lax.rem(behind, 2)),
     ]
-    step_two = [
-        move(MOVE + 2, x_via.at[0], x_move.at[0], y, down, lax.div(x, 2)),
-        move(MOVE + 3, x_via.at[1], x_move.at[1], down, x, k),
-    ]
+    step_two = []
+    for h in range(2):
+        rows = pl.ds(h * hsub, hsub)
+        step_two += [
+            move(MOVE + 2 + h, x_via.at[0, rows], x_move.at[0, rows], y, down, lax.div(x, 2)),
+            move(MOVE + 4 + h, x_via.at[1, rows], x_move.at[1, rows], down, x, k),
+        ]
     out_left = pltpu.make_async_copy(x_via.at[0], x_out.at[0], load_sem.at[0])
     out_right = pltpu.make_async_copy(x_move.at[1], x_out.at[1], load_sem.at[1])
 
@@ -418,6 +421,11 @@
         for n, copy in zip(ORDER, fwd_a):
             send_a[n].wait_recv()
             copy.start()
+
+        @pl.when(p == SWEEPS)
+        def _():
+            start_moves(*step_two[2:])
+
         phase("mm_near1")
         loaded(loads_a[1])
         loaded(loads_a[2])
@@ -690,7 +698,7 @@
         @pl.when(jnp.logical_and(last, q == 1))
         def _():
             end_moves(*step_one)
-            start_moves(*step_two)
+            start_moves(*step_two[:2])
 
         phase("chol")
 

time: 353 us -> 351 us (level)
  no operation moved by 1% of the time
where the time goes in v1:
time: 351 us
  Pallas kernels  350 us (100%)
    pallas_call x1, Pallas kernels, local_program(): pl.pallas_call(functools.partial(kernel, (nrow, ncol, rows * nrow)), out_...  348 us

profile of v1, /device:TPU:97, one launch (start us, length us, event | category | flops | bytes accessed | tf_op | source)
XLA Modules:
  0.0 351.2 jit_solution(3940642984466849523)
XLA Ops:
  0.6 348.3 %subspace.1 = (f32[2,512,256]{2,1,0:T(8,128)}, f32[2,256,256]{2,1,0:T(8,128)}) custom-call(bf16[4096,2048]{1,0:T(8,128)(2,1)} %left_op.1, f32[512,256]{1,0:T(8,128)} %left_start.1, bf16[4096,2048]{1,0:T(8,128)(2,1)} %right_op.1, f32[512,256]{1,0:T(8,128)} %right_start.1), custom_call_target="tpu_custom_call" | custom-call | tf_op jit(solution)/shard_map/subspace/pallas_call | solution.py:827
  348.9 2.2 hand_over.1

commit v2 on v1

--- a/solution.py
+++ b/solution.py
@@ -106,7 +106,7 @@
         data = {
             t: [work[pl.ds(first + GROUP * g, GROUP), t * tile : (t + 1) * tile] for g in range(groups)] for t in tiles
         }
-        pivots = [jnp.ones(full, F32) for _ in range(groups)]
+        roots = [jnp.ones(full, F32) for _ in range(groups)]
         def spread_columns(start, end):
             at = first - near * tile
             return {
@@ -120,30 +120,24 @@
                 cols |= spread_columns(STEP, PIVOTS)
             gj, rj = divmod(j, GROUP)
             col = cols[j]
-            pivot = lane(col[gj][rj : rj + 1])
-            inv = 1.0 / pivot
-            pivots[gj] = jnp.where(sub == rj, pivot, pivots[gj])
+            root = lax.rsqrt(lane(col[gj][rj : rj + 1]))
+            roots[gj] = jnp.where(sub == rj, root, roots[gj])
+            low = {g: col[g] * root for g in range(gj, groups)}
             for nxt in range(j + 1, PIVOTS if j >= STEP - AHEAD else STEP):
                 gn, rn = divmod(nxt, GROUP)
-                entry = lane(col[gn][rn : rn + 1])
-                if nxt == j + 1:
-                    for g in range(gn, groups):
-                        cols[nxt][g] = cols[nxt][g] - (col[g] * entry) * inv
-                else:
-                    scaled = entry * inv
-                    for g in range(gn, groups):
-                        cols[nxt][g] = cols[nxt][g] - col[g] * scaled
+                entry = lane(col[gn][rn : rn + 1]) * root
+                for g in range(gn, groups):
+                    cols[nxt][g] = cols[nxt][g] - low[g] * entry
             for g in range(gj, groups):
-                factor = col[g] * inv
+                factor = low[g] * root
                 if g == gj:
                     if rj == GROUP - 1:
                         continue
                     factor = jnp.where(sub > rj, factor, 0.0)
                 for t in tiles:
                     data[t][g] = data[t][g] - factor * lane(data[t][gj][rj : rj + 1])
-        scale = [lax.rsqrt(p) for p in pivots]
         for t in tiles:
-            data[t] = [d * s for d, s in zip(data[t], scale, strict=True)]
+            data[t] = [d * s for d, s in zip(data[t], roots, strict=True)]
         for t in tiles:
             if t >= 2:
                 for g in range(groups):

time: 351 us -> 352 us (level)
  no operation moved by 1% of the time
where the time goes in v2:
time: 352 us
  Pallas kernels  351 us (100%)
    pallas_call x1, Pallas kernels, local_program(): pl.pallas_call(functools.partial(kernel, (nrow, ncol, rows * nrow)), out_...  349 us

profile of v2, /device:TPU:97, one launch (start us, length us, event | category | flops | bytes accessed | tf_op | source)
XLA Modules:
  0.0 352.0 jit_solution(13640047747017644075)
XLA Ops:
  0.6 349.0 %subspace.1 = (f32[2,512,256]{2,1,0:T(8,128)}, f32[2,256,256]{2,1,0:T(8,128)}) custom-call(bf16[4096,2048]{1,0:T(8,128)(2,1)} %left_op.1, f32[512,256]{1,0:T(8,128)} %left_start.1, bf16[4096,2048]{1,0:T(8,128)(2,1)} %right_op.1, f32[512,256]{1,0:T(8,128)} %right_start.1), custom_call_target="tpu_custom_call" | custom-call | tf_op jit(solution)/shard_map/subspace/pallas_call | solution.py:821
  349.6 2.2 hand_over.1

commit v3 on v2

--- a/solution.py
+++ b/solution.py
@@ -21,8 +21,8 @@
 NT = (((1,), (1,)), ((), ()))
 
 SLOTS = 8
-KINDS = range(0, 17 * SLOTS, SLOTS)
-AG_T, AG_A, AG_B, RELAY, RELAY_A, RS_T, RS_A, PAIR, GRAM_PAIR, GRAM_RS, GRAM_AG, LINV, MOVE, START, SWAP_Y, SWAP_H, DIAGONAL = KINDS
+KINDS = range(0, 19 * SLOTS, SLOTS)
+AG_T, AG_A, AG_B, RELAY, RELAY_A, RS_T, RS_A, PAIR, GRAM_PAIR, GRAM_RS, GRAM_AG, LINV, MOVE, START, SWAP_Y, SWAP_H, DIAGONAL, ON_T, ON_A = KINDS
 ORDER = (0, 2, 1, 3)
 OFFSETS = sorted(
     ((dy, dx) for dy in range(RING) for dx in range(RING) if dy or dx),
@@ -191,13 +191,15 @@
 
     phase = Phases()
     phase("boot")
+    def routes():
+        for dy, dx in OFFSETS:
+            to_y, to_x = (y, yp, yf, ym)[dy], (x, xp, xf, xm)[dx]
+            yield dy * RING + dx, to_y * RING + to_x, to_y, to_x
+
     barrier = pltpu.get_barrier_semaphore()
-    here = y * ncol + c
-    for o in range(1, nrow * ncol):
-        there = lax.rem(here + o, nrow * ncol)
-        pl.semaphore_signal(
-            barrier, inc=1, device_id={"row": lax.div(there, ncol), "col": lax.rem(there, ncol)}, device_id_type=pl.DeviceIdType.MESH
-        )
+    peers = [dev(to_y, to_x, core) for _, _, to_y, to_x in routes() for core in range(CORES)] + [partner]
+    for peer in peers:
+        pl.semaphore_signal(barrier, inc=1, device_id=peer, device_id_type=pl.DeviceIdType.MESH)
 
     starts = [
         pltpu.make_async_copy(left_start, ycur.at[0], load_sem.at[8]),
@@ -244,7 +246,7 @@
         ag_t[x, h, k] = ycur[0, h * hsub : (h + 1) * hsub].T.astype(BF16)
     for h in range(2):
         x_half[0, h] = ycur[1, h * hsub : (h + 1) * hsub].astype(BF16)
-    pl.semaphore_wait(barrier, nrow * ncol - 1)
+    pl.semaphore_wait(barrier, len(peers))
     first_one = [move(MOVE + h, x_half.at[0, h], x_half.at[1, h], up, x, k) for h in range(2)]
     first_two = [move(MOVE + 2 + h, x_half.at[1, h], ag_a.at[y, h], y, down, lax.div(x, 2)) for h in range(2)]
     start_moves(*first_one)
@@ -256,15 +258,20 @@
     def piece_t(chip, h):
         return ag_t.at[chip, h]
 
+    def start_all(copies):
+        for n in ORDER:
+            for copy in copies[n]:
+                copy.start()
+
     def gather_t():
         to_p, to_m = dev(y, xp, k), dev(y, xm, k)
-        sends = [
-            push(AG_T + n, piece_t(x, h), piece_t(x, h), to) for n, (h, to) in enumerate(((0, to_p), (1, to_p), (1, to_m), (0, to_m)))
-        ]
-        onward = [
-            push(AG_T + 4, piece_t(xm, 0), piece_t(xm, 0), to_p),
-            push(AG_T + 5, piece_t(xp, 1), piece_t(xp, 1), to_m),
-        ]
+
+        def parts(kind, n, chip, h, to):
+            pieces = [ag_t.at[chip, h, core] for core in (k, other)]
+            return [push(kind + CORES * n + part, piece, piece, to) for part, piece in enumerate(pieces)]
+
+        sends = [parts(AG_T, n, x, h, to) for n, (h, to) in enumerate(((0, to_p), (1, to_p), (1, to_m), (0, to_m)))]
+        onward = [parts(ON_T, 0, xm, 0, to_p), parts(ON_T, 1, xp, 1, to_m)]
         relays = [push(RELAY, ag_t.at[x], ag_t.at[x], partner)] + [
             push(RELAY + 1 + n, piece_t(i, h), piece_t(i, h), partner)
             for n, (i, h) in enumerate(((xm, 0), (xp, 1), (xm, 1), (xp, 0), (xf, 0), (xf, 1)))
@@ -272,19 +279,20 @@
         return sends, onward, relays
 
     def gather_a():
+        def parts(kind, took, n, src, i, h, row, core):
+            pieces = [pl.ds(part * hsub // 2, hsub // 2) for part in range(2)]
+            return [
+                pltpu.make_async_remote_copy(
+                    src_ref=src.at[h, rows], dst_ref=ag_a.at[i, h, rows], send_sem=send.at[kind + 2 * n + part],
+                    recv_sem=recv.at[took + 2 * n + part], device_id=dev(row, x, core), device_id_type=pl.DeviceIdType.MESH,
+                )
+                for part, rows in enumerate(pieces)
+            ]
+
         routes = ((0, yp), (1, yp), (1, ym), (0, ym))
-        sends = [push(AG_A + n, ag_a.at[y, h], ag_a.at[y, h], dev(i, x, k)) for n, (h, i) in enumerate(routes)]
-        onward = [
-            push(AG_A + 4, ag_a.at[ym, 0], ag_a.at[ym, 0], dev(yp, x, k)),
-            push(AG_A + 5, ag_a.at[yp, 1], ag_a.at[yp, 1], dev(ym, x, k)),
-        ]
-        for_other = [
-            pltpu.make_async_remote_copy(
-                src_ref=x_half.at[0, h], dst_ref=ag_a.at[y, h], send_sem=send.at[AG_B + n], recv_sem=recv.at[AG_A + n],
-                device_id=dev(i, x, other), device_id_type=pl.DeviceIdType.MESH,
-            )
-            for n, (h, i) in enumerate(routes)
-        ]
+        sends = [parts(AG_A, AG_A, n, ag_a.at[y], y, h, row, k) for n, (h, row) in enumerate(routes)]
+        for_other = [parts(AG_B, AG_A, n, x_half.at[0], y, h, row, other) for n, (h, row) in enumerate(routes)]
+        onward = [parts(ON_A, ON_A, 0, ag_a.at[ym], ym, 0, yp, k), parts(ON_A, ON_A, 1, ag_a.at[yp], yp, 1, ym, k)]
         return sends, onward, for_other, push(RELAY_A, x_half.at[0], ag_a.at[y], partner)
 
     def ring_scatter(base, part, got, plus, minus, far, to):
@@ -364,8 +372,7 @@
 
             @pl.when(drives_t)
             def _():
-                for n in ORDER:
-                    send_t[n].start()
+                start_all(send_t)
 
         @pl.when(p > 0)
         def _():
@@ -386,23 +393,27 @@
 
         @pl.when(p == 0)
         def _():
-            end_moves(first_two[0])
-            send_a[0].start()
-            send_a[3].start()
-            end_moves(first_two[1])
-            send_a[2].start()
-            send_a[1].start()
+            for h, copies in enumerate(((send_a[0], send_a[3]), (send_a[2], send_a[1]))):
+                end_moves(first_two[h])
+                for copy in copies[0] + copies[1]:
+                    copy.start()
             loads_a[0].wait()
             for owner in range(RING * CORES):
                 mm_a(own_y, owner, True)
 
-        def take_t(arrived, then):
+        def take(arrived, onward=(), relays=()):
+            for part in range(2):
+                for n, copies in enumerate(arrived):
+                    copies[part].wait_recv()
+                    for copies in onward[n : n + 1]:
+                        copies[part].start()
+            for copy in relays:
+                copy.start()
+
+        def take_t(*args):
             @pl.when(drives_t)
             def _():
-                for copy, follow in zip(arrived, then):
-                    copy.wait_recv()
-                    for nxt in follow:
-                        nxt.start()
+                take(*args)
 
         def relayed(*copies):
             @pl.when(jnp.logical_not(drives_t))
@@ -411,10 +422,8 @@
                     copy.wait_recv()
 
         phase("ag_wait1")
-        take_t([send_t[n] for n in ORDER[:2]], zip(fwd_t, relays[1:3]))
-        for n, copy in zip(ORDER, fwd_a):
-            send_a[n].wait_recv()
-            copy.start()
+        take_t([send_t[n] for n in ORDER[:2]], fwd_t, relays[1:3])
+        take([send_a[n] for n in ORDER[:2]], fwd_a)
 
         @pl.when(p == SWEEPS)
         def _():
@@ -431,18 +440,16 @@
         for owner in range(RING):
             mm_t([(xm, 0), (xp, 1)], owner)
         phase("mm_near2")
-        take_t([send_t[n] for n in ORDER[2:]], zip(relays[3:5]))
-        for n in ORDER[2:]:
-            send_a[n].wait_recv()
+        take_t([send_t[n] for n in ORDER[2:]], (), relays[3:5])
+        take([send_a[n] for n in ORDER[2:]])
         for owner in range(RING * CORES):
             mm_a([(ym, 1), (yp, 0)], owner)
         relayed(*relays[3:5])
         for owner in range(RING):
             mm_t([(xm, 1), (xp, 0)], owner)
         phase("ag_far")
-        take_t(fwd_t, zip(relays[5:]))
-        for copy in fwd_a:
-            copy.wait_recv()
+        take_t(fwd_t, (), relays[5:])
+        take(fwd_a)
         phase("mm_far")
 
         loaded(loads_a[3])
@@ -528,12 +535,12 @@
         ycur[a, 0:hsub] = p_a[kk, 0:hsub] + r_a[3] + r_a[4]
         ycur[a, hsub:sub] = p_a[kk, hsub:sub] + r_a[2] + r_a[5]
         phase("rs_drain")
-        for copy in fwd_a + pairs + out_t + out_a:
+        for copy in sum(fwd_a, pairs + out_t + out_a):
             copy.wait_send()
 
         @pl.when(drives_t)
         def _():
-            for copy in send_t + fwd_t + relays[1:]:
+            for copy in sum(send_t + fwd_t, relays[1:]):
                 copy.wait_send()
 
             @pl.when(p > 0)
@@ -542,20 +549,15 @@
 
         @pl.when(jnp.logical_or(p == 0, drives_a))
         def _():
-            for copy in send_a:
+            for copy in sum(send_a, []):
                 copy.wait_send()
 
         @pl.when(jnp.logical_and(p > 0, drives_a))
         def _():
-            for copy in send_b + [relay_a]:
+            for copy in sum(send_b, [relay_a]):
                 copy.wait_send()
 
         phase()
-
-    def routes():
-        for dy, dx in OFFSETS:
-            to_y, to_x = (y, yp, yf, ym)[dy], (x, xp, xf, xm)[dx]
-            yield dy * RING + dx, to_y * RING + to_x, to_y, to_x
 
     def pair_of(rows):
         return push(GRAM_PAIR, g_loc.at[other, pl.ds(0, rows)], g_pair.at[pl.ds(0, rows)], partner)
@@ -732,8 +734,12 @@
             for i, core in enumerate((k, other)):
                 for h, rows in enumerate(new_x(i)):
                     ag_t[x, h, core] = rows.T.astype(BF16)
-            for n in ORDER:
-                sends[n].start()
+
+                for n in ORDER[:2]:
+                    sends[n][i].start()
+            for n in ORDER[2:]:
+                for copy in sends[n]:
+                    copy.start()
             relays[0].start()
 
         @pl.when(k != t)
@@ -741,12 +747,10 @@
             sends, _, for_other, relay_a = gather_a()
             for h, rows in enumerate(new_x(0)):
                 ag_a[y, h] = rows.astype(BF16)
-            for n in ORDER:
-                sends[n].start()
+            start_all(sends)
             for h, rows in enumerate(new_x(1)):
                 x_half[0, h] = rows.astype(BF16)
-            for n in ORDER:
-                for_other[n].start()
+            start_all(for_other)
             relay_a.start()
 
         phase()

time: 352 us -> 352 us (level)
  no operation moved by 1% of the time
where the time goes in v3:
time: 352 us
  Pallas kernels  351 us (100%)
    pallas_call x1, Pallas kernels, local_program(): pl.pallas_call(functools.partial(kernel, (nrow, ncol, rows * nrow)), out_...  349 us

profile of v3, /device:TPU:97, one launch (start us, length us, event | category | flops | bytes accessed | tf_op | source)
XLA Modules:
  0.0 351.8 jit_solution(10141795363387238617)
XLA Ops:
  0.6 348.8 %subspace.1 = (f32[2,512,256]{2,1,0:T(8,128)}, f32[2,256,256]{2,1,0:T(8,128)}) custom-call(bf16[4096,2048]{1,0:T(8,128)(2,1)} %left_op.1, f32[512,256]{1,0:T(8,128)} %left_start.1, bf16[4096,2048]{1,0:T(8,128)(2,1)} %right_op.1, f32[512,256]{1,0:T(8,128)} %right_start.1), custom_call_target="tpu_custom_call" | custom-call | tf_op jit(solution)/shard_map/subspace/pallas_call | solution.py:825
  349.5 2.2 hand_over.1
